TPU v7x, 32 devices: a whole 2x2x4 slice. The times are simulated.
32 devices in a mesh: zero: 8 (over z, x), model: 4 (over y, core).
Axes of the slice: x: 2, y: 2, z: 4, core: 2. Of those that a mesh axis runs over, the one named last changes fastest.
Arguments:
- w_query: bfloat16 [4096, 4096], P('zero', 'model'), may hold values from -0.125 to 0.125
- low_query: bfloat16 [4096, 16], P('zero'), may hold values from -0.09375 to 0.09375
- high_query: bfloat16 [16, 4096], P(None, 'model'), may hold values from -1.5 to 1.5
- w_key: bfloat16 [4096, 4096], P('zero', 'model'), may hold values from -0.125 to 0.125
- low_key: bfloat16 [4096, 16], P('zero'), may hold values from -0.09375 to 0.09375
- high_key: bfloat16 [16, 4096], P(None, 'model'), may hold values from -1.5 to 1.5
- w_value: bfloat16 [4096, 4096], P('zero', 'model'), may hold values from -0.125 to 0.125
- low_value: bfloat16 [4096, 16], P('zero'), may hold values from -0.09375 to 0.09375
- high_value: bfloat16 [16, 4096], P(None, 'model'), may hold values from -1.5 to 1.5
- norm_train: float32 [4096], P(('zero', 'model')), may hold values from 0.25 to 1.75
- norm_step: float32 [4096], P(('zero', 'model')), may hold values from -0.3 to 0.3
Outputs:
- serving_query: bfloat16 [4096, 4096], P(None, 'model')
- serving_key: bfloat16 [4096, 4096], P(None, 'model')
- serving_value: bfloat16 [4096, 4096], P(None, 'model')
- factor_query: float32 [4096], P('model')
- factor_key: float32 [4096], P('model')
- factor_value: float32 [4096], P('model')
- serve_norm: bfloat16 [4096], replicated
All inputs are finite; a program needn't handle non-finite values. Where the computation divides by a largest or mean magnitude, that divisor is 1e-20 or more.
Results may differ from a plain program's by a relative error of at most 0.001.
Values may be sent and summed in bfloat16 or wider, within the bound.
A program may use at most 128 MiB of HBM per device.

v0:
```python
import jax
import jax.numpy as jnp
from jax import lax
from jax.sharding import PartitionSpec as P

D_MODEL = 4096


mix_rate = 0.5


def per_device(
    w_query,
    low_query,
    high_query,
    w_key,
    low_key,
    high_key,
    w_value,
    low_value,
    high_value,
    norm_train,
    norm_step,
):
    whole_query = w_query.astype(jnp.float32) + mix_rate * jnp.dot(
        low_query, high_query, preferred_element_type=jnp.float32
    )
    whole_key = w_key.astype(jnp.float32) + mix_rate * jnp.dot(
        low_key, high_key, preferred_element_type=jnp.float32
    )
    whole_value = w_value.astype(jnp.float32) + mix_rate * jnp.dot(
        low_value, high_value, preferred_element_type=jnp.float32
    )
    total_query, total_key, total_value = lax.psum(
        (
            jnp.sum(jnp.abs(whole_query), axis=0),
            jnp.sum(jnp.abs(whole_key), axis=0),
            jnp.sum(jnp.abs(whole_value), axis=0),
        ),
        "zero",
    )
    factor_query = total_query / D_MODEL
    factor_key = total_key / D_MODEL
    factor_value = total_value / D_MODEL
    narrow_query, narrow_key, narrow_value = (
        (whole_query / factor_query).astype(jnp.bfloat16),
        (whole_key / factor_key).astype(jnp.bfloat16),
        (whole_value / factor_value).astype(jnp.bfloat16),
    )
    serving_query, serving_key, serving_value = (
        lax.all_gather(narrow_query, "zero", axis=0, tiled=True),
        lax.all_gather(narrow_key, "zero", axis=0, tiled=True),
        lax.all_gather(narrow_value, "zero", axis=0, tiled=True),
    )
    serve_norm = lax.all_gather(
        (norm_train + norm_step).astype(jnp.bfloat16), ("zero", "model"), axis=0, tiled=True
    )
    return (
        serving_query,
        serving_key,
        serving_value,
        factor_query,
        factor_key,
        factor_value,
        serve_norm,
    )


def solution(mesh):
    placed = (
        P("zero", "model"),
        P("zero", None),
        P(None, "model"),
        P("zero", "model"),
        P("zero", None),
        P(None, "model"),
        P("zero", "model"),
        P("zero", None),
        P(None, "model"),
        P(("zero", "model")),
        P(("zero", "model")),
    )
    return jax.shard_map(
        per_device,
        mesh=mesh,
        in_specs=placed,
        out_specs=(
            P(None, "model"),
            P(None, "model"),
            P(None, "model"),
            P("model"),
            P("model"),
            P("model"),
            P(),
        ),
        check_vma=False,
    )
```

profile of v0, /device:TPU:0, one launch (start us, length us, event | category | flops | bytes accessed | tf_op | source)
XLA Modules:
  0.0 457.2 jit_solution(10498618471171676512)
XLA Ops:
  7.2 0.0 copy-start
  7.2 0.0 copy-start.1
  7.2 0.0 copy-start.5
  7.2 0.0 copy-start.3
  7.2 0.0 all-gather.7.cloned.1.call-start
  7.3 0.7 copy-done
  7.9 1.8 abs_reduce_fusion.2
  9.7 0.0 copy-done.1
  9.7 0.0 copy-done.5
  9.7 0.0 copy-done.3
  9.8 0.0 copy-start.2
  9.8 0.0 copy-start.4
  9.8 0.0 copy-start.6
  9.8 1.8 abs_reduce_fusion.1
  11.6 0.0 copy-done.2
  11.6 0.0 copy-done.4
  11.6 0.0 copy-done.6
  11.6 1.8 abs_reduce_fusion
  13.5 38.8 %all-reduce = (f32[1024]{0:T(1024)S(1)}, f32[1024]{0:T(1024)S(1)}, f32[1024]{0:T(1024)S(1)}) all-reduce(f32[1024]{0:T(1024)S(1)} %get-tuple-element.10, f32[1024]{0:T(1024)S(1)} %get-tuple-element.12, f32[1024]{0:T(1024)S(1)} %get-tuple-element.14), channel_id=1, replica_groups=mesh['zero'=8,'model'=4] {'zero'}, use_global_device_ids=true, to_apply=%region_1.0 | all-reduce | flops 3072 | bytes 24576 | tf_op jit(solution)/shard_map/psum | solution.py:34
  52.3 0.0 copy-start.7
  52.3 2.8 divide_convert_fusion.1
  55.1 0.0 all-gather.7.cloned.1.call-update
  55.2 0.0 copy-done.7
  55.2 0.0 all-gather.9.cloned.1.call-start
  55.2 0.0 copy-start.8
  55.2 2.9 divide_convert_fusion
  58.2 0.0 all-gather.9.cloned.1.call-update
  58.2 0.0 copy-done.8
  58.2 0.0 all-gather.5.cloned.1.call-start
  58.3 0.0 copy-start.9
  58.3 0.0 copy-start.10
  58.3 0.0 copy-start.11
  58.3 1.2 divide_convert_fusion.2
  59.5 0.0 all-gather.5.cloned.1.call-update
  59.6 0.0 copy-done.9
  59.6 0.0 copy-done.10
  59.6 0.0 copy-done.11
  59.6 39.3 %all-gather = bf16[32,1,128]{2,1,0:T(2,128)(2,1)S(1)} all-gather(bf16[1,1,128]{2,1,0:T(2,128)(2,1)S(1)} %convert_bitcast_fusion), channel_id=1, replica_groups=mesh['zero'=8,'model'=4] {'zero','model'}, dimensions={0}, use_global_device_ids=true | all-gather | bytes 8448 | tf_op jit(solution)/shard_map/all_gather | solution.py:55
  98.9 0.6 reduce
  99.5 77.6 %all-gather.7.cloned.1.call-done = bf16[4096,1024]{1,0:T(8,128)(2,1)} async-done(((bf16[512,1024]{1,0:T(8,128)(2,1)}), bf16[4096,1024]{1,0:T(8,128)(2,1)}) %all-gather.7.cloned.1.call-update) | async-done | bytes 8388624 | tf_op jit(solution)/shard_map/all_gather | solution.py:52
  177.1 124.8 %all-gather.9.cloned.1.call-done = bf16[4096,1024]{1,0:T(8,128)(2,1)} async-done(((bf16[512,1024]{1,0:T(8,128)(2,1)}), bf16[4096,1024]{1,0:T(8,128)(2,1)}) %all-gather.9.cloned.1.call-update) | async-done | bytes 8388624 | tf_op jit(solution)/shard_map/all_gather | solution.py:53
  302.0 125.4 %all-gather.5.cloned.1.call-done = bf16[4096,1024]{1,0:T(8,128)(2,1)} async-done(((bf16[512,1024]{1,0:T(8,128)(2,1)}), bf16[4096,1024]{1,0:T(8,128)(2,1)}) %all-gather.5.cloned.1.call-update) | async-done | bytes 8388624 | tf_op jit(solution)/shard_map/all_gather | solution.py:51
  427.4 7.8 %copy.21 = bf16[4096,1024]{1,0:T(8,128)(2,1)} copy(bf16[4096,1024]{1,0:T(8,128)(2,1)} %all-gather.5.cloned.1.call-done) | data formatting | bytes 16777216
  435.1 7.8 %copy.22 = bf16[4096,1024]{1,0:T(8,128)(2,1)} copy(bf16[4096,1024]{1,0:T(8,128)(2,1)} %all-gather.7.cloned.1.call-done) | data formatting | bytes 16777216
  442.9 7.8 %copy.23 = bf16[4096,1024]{1,0:T(8,128)(2,1)} copy(bf16[4096,1024]{1,0:T(8,128)(2,1)} %all-gather.9.cloned.1.call-done) | data formatting | bytes 16777216
  (4 shorter events, 0.0 us)
Async XLA Ops:
  7.2 0.8 copy-start
  7.2 2.5 copy-start.1
  7.2 2.5 copy-start.5
  7.2 2.5 copy-start.3
  7.2 169.9 %all-gather.7.cloned.1.call-start = ((), (), s32[]{:S(2)}) async-start(), calls=%async_computation.1 | async-start | bytes 9437184 | tf_op jit(solution)/shard_map/all_gather | solution.py:52
  9.8 1.9 copy-start.2
  9.8 1.9 copy-start.4
  9.8 1.9 copy-start.6
  52.3 2.8 copy-start.7
  55.2 246.8 %all-gather.9.cloned.1.call-start = ((), (), s32[]{:S(2)}) async-start(), calls=%async_computation.2 | async-start | bytes 9437184 | tf_op jit(solution)/shard_map/all_gather | solution.py:53
  55.2 3.0 copy-start.8
  58.2 369.2 %all-gather.5.cloned.1.call-start = ((), (), s32[]{:S(2)}) async-start(), calls=%async_computation | async-start | bytes 9437184 | tf_op jit(solution)/shard_map/all_gather | solution.py:51
  58.3 1.3 copy-start.9
  58.3 1.3 copy-start.10
  58.3 1.3 copy-start.11
Sparse Core Ops, SparseCore 0:
  55.3 121.8 all-gather.6
  179.3 122.6 all-gather.8
  304.7 122.6 all-gather.4
where the time goes:
time: 458 us; the launch traced here: 457 us
  waiting for transfers between devices  328 us (72%)
  blocking collectives  78.1 us (17%)
  local copies, waits for them, and re-layouts  24 us (5%)
  between operations  13.9 us (3%)
  other arithmetic  7.63 us (2%)
  matrix products  5.47 us (1%)
    all_gather x1, waiting for transfers between devices, per_device(): lax.all_gather(narrow_query, 'zero', axis=0, tiled=True)  125 us
    all_gather x1, waiting for transfers between devices, per_device(): lax.all_gather(narrow_value, 'zero', axis=0, tiled=True)  125 us
    all_gather x1, waiting for transfers between devices, per_device(): lax.all_gather(narrow_key, 'zero', axis=0, tiled=True)  77.6 us
    all_gather x1, blocking collectives, per_device(): lax.all_gather((norm_train + norm_step).astype(jnp.bfloat16), ('zero', 'm...  39.3 us
    psum x1, blocking collectives, per_device(): lax.psum((jnp.sum(jnp.abs(whole_query), axis=0), jnp.sum(jnp.abs(whole_ke...  38.8 us
    unnamed x27, local copies, waits for them, and re-layouts  24 us
  transfers between devices with their start and end apart: 3, of which 3 were waited for; matrix products, arithmetic and copies ran while one was open for 1% of the time, Pallas kernels for 0%

commit v1 on v0

v1 whole, which is shorter than its diff:
```python
import functools

import jax
import jax.numpy as jnp
from jax import lax
from jax.experimental import pallas as pl
from jax.experimental.pallas import tpu as pltpu
from jax.sharding import PartitionSpec as P

MESH = pl.DeviceIdType.MESH
mix_rate = 0.5
COLUMNS = 2
PIECES = 6
EXTRAS = 2


def queues_of(z, length):
    every = list(range(PIECES + EXTRAS))
    late = list(range(PIECES // 2, PIECES))
    early = [c for c in every if c not in late]
    out = {"up": [], "down": [], "side": []}
    if z < length - 1:
        out["up"] += [(z - s, 0, c) for s in range(z + 1) for c in every]
        if z == 0:
            out["up"] += [(0, 1, c) for c in every]
        if z == length - 2:
            out["up"] += [(z, 1, c) for c in late]
    if z > 0:
        out["down"] += [(z + s, 0, c) for s in range(length - z) for c in every]
        if z == length - 1:
            out["down"] += [(z, 1, c) for c in every]
        if z == 1:
            out["down"] += [(z, 1, c) for c in late]
    for b in sorted(range(length), key=lambda b: (abs(b - z), b)):
        pieces = every
        if (z, b) in ((0, 1), (length - 1, length - 2)):
            pieces = early
        if (z, b) in ((1, 0), (length - 2, length - 1)):
            pieces = []
        out["side"] += [(b, 0, c) for c in pieces]
    return out


def order_of(length):
    size = [1.0] * PIECES + [0.1, 0.03]
    queues = [queues_of(z, length) for z in range(length)]
    far = 1e9
    there = [{} for _ in range(length)]
    for z in range(length):
        for c in range(PIECES + EXTRAS):
            there[z][z, 0, c] = 0.0 if c < PIECES else 1.0
    for _ in range(4 * length):
        for z in range(length):
            for name, queue in queues[z].items():
                now = 0.0
                for b, o, c in queue:
                    now = max(now, there[z].get((b, o, c), far)) + size[c]
                    to = {"up": z + 1, "down": z - 1, "side": z}[name]
                    key = (b, 1 - o if name == "side" else o, c)
                    there[to][key] = now
    result = []
    for z in range(length):
        events = []
        for name, queue in queues[z].items():
            key = 0.0
            for at, (b, o, c) in enumerate(queue):
                key = max(key, there[z][b, o, c])
                events.append((key, at, name, b, o, c))
        result.append(sorted(events))
        assert max(e[0] for e in events) < far
    return result


def gather_kernel(
    n_zero, n_model,
    w_q, w_k, w_v, l_q, l_k, l_v, h_q, h_k, h_v, n_a, n_b,
    g_q, g_k, g_v, lows, sums, norms,
    w_vm, h_vm, lt_vm, ps_vm, na_vm, nb_vm, ns_vm,
    send_sem, recv_sem, load_sem, store_sem, nsend_sem, nrecv_sem,
):
    w, low, high, gathered = (w_q, w_k, w_v), (l_q, l_k, l_v), (h_q, h_k, h_v), (g_q, g_k, g_v)
    length = n_zero // COLUMNS
    zero, model = lax.axis_index("zero"), lax.axis_index("model")
    place, column = zero // COLUMNS, zero % COLUMNS
    rows, rank = w_q.shape[0], l_q.shape[0]
    half = rows // 2
    count = n_zero * n_model
    me = zero * n_model + model

    loads = []
    for m in range(3):
        loads.append(pltpu.make_async_copy(w[m], w_vm.at[m], load_sem.at[m]))
        into = lt_vm.at[pl.ds(m * rank, rank)]
        loads.append(pltpu.make_async_copy(low[m], into, load_sem.at[3 + m]))
        loads.append(pltpu.make_async_copy(high[m], h_vm.at[m], load_sem.at[6 + m]))
    loads.append(pltpu.make_async_copy(n_a, na_vm, load_sem.at[9]))
    loads.append(pltpu.make_async_copy(n_b, nb_vm, load_sem.at[10]))
    for load in loads:
        load.start()

    barrier = pltpu.get_barrier_semaphore()

    def greet(k, carry):
        to = lax.rem(me + k, count)
        pl.semaphore_signal(
            barrier, inc=1, device_id=(to // n_model, to % n_model), device_id_type=MESH
        )
        return carry

    lax.fori_loop(1, count, greet, 0)
    pl.semaphore_wait(barrier, count - 1)

    def block_at(b, o):
        return b * COLUMNS + (column if o == 0 else 1 - column)

    def landing(block, c):
        if c < PIECES:
            first = pl.multiple_of(block * rows, rows) + (c % 2) * half
            return gathered[c // 2].at[pl.ds(pl.multiple_of(first, half), half)]
        return (lows, sums)[c - PIECES].at[block]

    lane_of = {"up": 0, "down": 1, "side": 2}

    def copy_of(z, name, at, b, o, c):
        block = block_at(b, o)
        target = {
            "up": (z + 1) * COLUMNS + column,
            "down": (z - 1) * COLUMNS + column,
            "side": z * COLUMNS + 1 - column,
        }[name]
        own = b == z and o == 0
        if own and c < PIECES:
            source = w[c // 2].at[pl.ds((c % 2) * half, half)]
        elif own:
            source = (lt_vm, ps_vm)[c - PIECES]
        else:
            source = landing(block, c)
        return pltpu.make_async_remote_copy(
            src_ref=source,
            dst_ref=landing(block, c),
            send_sem=send_sem.at[lane_of[name], at],
            recv_sem=recv_sem.at[block, c],
            device_id=(target, model),
            device_id_type=MESH,
        )

    def arrival(b, o, c):
        block = block_at(b, o)
        return pltpu.make_async_copy(
            landing(block, c), landing(block, c), recv_sem.at[block, c]
        )

    orders = order_of(length)
    for z in range(length):

        @pl.when(place == z)
        def _(z=z):
            for key, at, name, b, o, c in orders[z]:
                if b == z and o == 0 and c < PIECES:
                    copy_of(z, name, at, b, o, c).start()

    for load in loads:
        load.wait()
    stores = []
    for m in range(3):
        into = gathered[m].at[pl.ds(pl.multiple_of(zero * rows, rows), rows)]
        stores.append(pltpu.make_async_copy(w_vm.at[m], into, store_sem.at[m]))
        stores[-1].start()
    ns_vm[...] = na_vm[...] + nb_vm[...]
    tile = 128
    for m in range(3):

        def add(i, total, m=m):
            at = pl.ds(pl.multiple_of(i * tile, tile), tile)
            mixed = lax.dot_general(
                lt_vm[m * rank : (m + 1) * rank, at],
                h_vm[m],
                (((0,), (0,)), ((), ())),
                preferred_element_type=jnp.float32,
            )
            whole = w_vm[m, at, :].astype(jnp.float32) + mix_rate * mixed
            return total + jnp.sum(
                jnp.abs(whole).reshape(tile // 8, 8, whole.shape[1]), axis=0
            )

        total = lax.fori_loop(
            0, rows // tile, add, jnp.zeros((8, w_vm.shape[2]), jnp.float32)
        )
        ps_vm[m : m + 1, :] = jnp.sum(total, axis=0, keepdims=True)

    def norm_copy(k):
        to = lax.rem(me + k, count)
        return pltpu.make_async_remote_copy(
            src_ref=ns_vm,
            dst_ref=norms.at[me],
            send_sem=nsend_sem.at[k],
            recv_sem=nrecv_sem.at[me],
            device_id=(to // n_model, to % n_model),
            device_id_type=MESH,
        )

    own = [
        pltpu.make_async_copy(lt_vm, lows.at[zero], store_sem.at[3]),
        pltpu.make_async_copy(ps_vm, sums.at[zero], store_sem.at[4]),
        pltpu.make_async_copy(ns_vm, norms.at[me], store_sem.at[5]),
    ]

    for z in range(length):

        @pl.when(place == z)
        def _(z=z):
            seen = set()
            for key, at, name, b, o, c in orders[z]:
                mine = b == z and o == 0
                if mine and c < PIECES:
                    continue
                if not mine and (b, o, c) not in seen:
                    seen.add((b, o, c))
                    arrival(b, o, c).wait()
                copy_of(z, name, at, b, o, c).start()
            for b in range(length):
                for o in range(2):
                    for c in range(PIECES + EXTRAS):
                        if (b, o) != (z, 0) and (b, o, c) not in seen:
                            arrival(b, o, c).wait()
            for key, at, name, b, o, c in orders[z]:
                copy_of(z, name, at, b, o, c).wait_send()

    for copy in own:
        copy.start()

    def send_norm(k, carry):
        norm_copy(k).start()
        return carry

    lax.fori_loop(1, count, send_norm, 0)
    for copy in stores + own:
        copy.wait()

    def end_norm(k, carry):
        norm_copy(k).wait_send()
        origin = lax.rem(me + k, count)
        pltpu.make_async_copy(norms.at[origin], norms.at[origin], nrecv_sem.at[origin]).wait()
        return carry

    lax.fori_loop(1, count, end_norm, 0)


def finish_kernel(d_model, g_q, g_k, g_v, lt, h_q, h_k, h_v, sums, s_q, s_k, s_v, f_q, f_k, f_v):
    rank = h_q.shape[0]
    for m, (g, h, s, f) in enumerate(
        ((g_q, h_q, s_q, f_q), (g_k, h_k, s_k, f_k), (g_v, h_v, s_v, f_v))
    ):
        factor = jnp.sum(sums[:, m, :], axis=0, keepdims=True) / d_model
        f[...] = factor
        scale = 1.0 / factor
        mixed = lax.dot_general(
            lt[0, m * rank : (m + 1) * rank, :],
            h[...],
            (((0,), (0,)), ((), ())),
            preferred_element_type=jnp.float32,
        )
        whole = g[...].astype(jnp.float32) + mix_rate * mixed
        s[...] = (whole * scale).astype(s.dtype)


def on_lines(n_zero, n_model, w_q, l_q, h_q, w_k, l_k, h_k, w_v, l_v, h_v, n_a, n_b):
    rows, width = w_q.shape
    rank = l_q.shape[1]
    d_model = rows * n_zero
    count = n_zero * n_model
    share = n_a.shape[0]
    sends = (n_zero // COLUMNS) * (PIECES + EXTRAS) + PIECES
    f32, bf16 = jnp.float32, jnp.bfloat16
    shape = jax.ShapeDtypeStruct
    anywhere = pl.BlockSpec(memory_space=pl.ANY)
    dma = pltpu.SemaphoreType.DMA
    g_q, g_k, g_v, lows, sums, norms = pl.pallas_call(
        functools.partial(gather_kernel, n_zero, n_model),
        out_shape=(
            shape((d_model, width), bf16),
            shape((d_model, width), bf16),
            shape((d_model, width), bf16),
            shape((n_zero, 3 * rank, rows), bf16),
            shape((n_zero, 3, width), f32),
            shape((count, 1, share), f32),
        ),
        in_specs=[anywhere] * 11,
        out_specs=(anywhere,) * 6,
        scratch_shapes=[
            pltpu.VMEM((3, rows, width), bf16),
            pltpu.VMEM((3, rank, width), bf16),
            pltpu.VMEM((3 * rank, rows), bf16),
            pltpu.VMEM((3, width), f32),
            pltpu.VMEM((1, share), f32),
            pltpu.VMEM((1, share), f32),
            pltpu.VMEM((1, share), f32),
            dma((3, sends)),
            dma((n_zero, PIECES + EXTRAS)),
            dma((11,)),
            dma((6,)),
            dma((count,)),
            dma((count,)),
        ],
        compiler_params=pltpu.CompilerParams(collective_id=0, has_side_effects=True),
    )(w_q, w_k, w_v, l_q.T, l_k.T, l_v.T, h_q, h_k, h_v, n_a.reshape(1, share), n_b.reshape(1, share))

    tile = rows // 2
    tall = pl.BlockSpec((tile, width), lambda i: (i, 0))
    wide = pl.BlockSpec((rank, width), lambda i: (0, 0))
    line = pl.BlockSpec((1, width), lambda i: (0, 0))
    s_q, s_k, s_v, f_q, f_k, f_v = pl.pallas_call(
        functools.partial(finish_kernel, d_model),
        grid=(d_model // tile,),
        out_shape=(shape((d_model, width), bf16),) * 3 + (shape((1, width), f32),) * 3,
        in_specs=[tall] * 3
        + [pl.BlockSpec((1, 3 * rank, tile), lambda i: (i // 2, 0, i % 2))]
        + [wide] * 3
        + [pl.BlockSpec((n_zero, 3, width), lambda i: (0, 0, 0))],
        out_specs=(tall,) * 3 + (line,) * 3,
        compiler_params=pltpu.CompilerParams(dimension_semantics=("arbitrary",)),
    )(g_q, g_k, g_v, lows, h_q, h_k, h_v, sums)
    norm = norms.astype(bf16).reshape(count * share)
    return (
        s_q, s_k, s_v, f_q.reshape(width), f_k.reshape(width), f_v.reshape(width), norm,
    )


def plain(n_zero, n_model, w_q, l_q, h_q, w_k, l_k, h_k, w_v, l_v, h_v, n_a, n_b):
    d_model = w_q.shape[0] * n_zero
    wholes = [
        w.astype(jnp.float32) + mix_rate * jnp.dot(l, h, preferred_element_type=jnp.float32)
        for w, l, h in ((w_q, l_q, h_q), (w_k, l_k, h_k), (w_v, l_v, h_v))
    ]
    totals = lax.psum([jnp.sum(jnp.abs(whole), axis=0) for whole in wholes], "zero")
    factors = [total / d_model for total in totals]
    serving = [
        lax.all_gather((whole / factor).astype(jnp.bfloat16), "zero", axis=0, tiled=True)
        for whole, factor in zip(wholes, factors)
    ]
    norm = lax.all_gather(
        (n_a + n_b).astype(jnp.bfloat16), ("zero", "model"), axis=0, tiled=True
    )
    return (*serving, *factors, norm)


def solution(mesh):
    n_zero, n_model = mesh.shape["zero"], mesh.shape["model"]
    lines = n_zero == 2 * n_model
    tall, low, wide = P("zero", "model"), P("zero", None), P(None, "model")
    return jax.shard_map(
        functools.partial(on_lines if lines else plain, n_zero, n_model),
        mesh=mesh,
        in_specs=(tall, low, wide) * 3 + (P(("zero", "model")),) * 2,
        out_specs=(wide,) * 3 + (P("model"),) * 3 + (P(),),
        check_vma=False,
    )
```

time: 458 us -> 284 us (0.62)
  waiting for transfers between devices: 328 us -> 0 us
  Pallas kernels: 0 us -> 282 us
  blocking collectives: 78.1 us -> 0 us
  local copies, waits for them, and re-layouts: 24 us -> 0.01 us
  between operations: 13.9 us -> 0.65 us
  other arithmetic: 7.63 us -> 0.65 us
  matrix products: 5.47 us -> 0 us
    all_gather x3 -> x0, waiting for transfers between devices: 328 us -> none  [the longest x1 125 us: per_device(): lax.all_gather(narrow_query, 'zero', axis=0, tiled=True)]
    pallas_call x0 -> x2, Pallas kernels: none -> 282 us  [the longest x1 257 us: on_lines(): pl.pallas_call(functools.partial(gather_kernel, n_zero, n_model), out_sha...]
    all_gather x1 -> x0, blocking collectives: 39.3 us -> none  [per_device(): lax.all_gather((norm_train + norm_step).astype(jnp.bfloat16), ('zero', 'm...]
    psum x1 -> x0, blocking collectives: 38.8 us -> none  [per_device(): lax.psum((jnp.sum(jnp.abs(whole_query), axis=0), jnp.sum(jnp.abs(whole_ke...]
    unnamed x27 -> x2, local copies, waits for them, and re-layouts: 24 us -> 0.01 us
    convert_element_type x3 -> x1, other arithmetic: 6.96 us -> 0.65 us  [on_lines(): norm = norms.astype(bf16).reshape(count * share)]
    dot_general x3 -> x0, matrix products: 5.47 us -> none  [the longest x1 1.84 us: per_device(): jnp.dot(low_key, high_key, preferred_element_type=jnp.float32)]
  transfers between devices with their start and end apart: 3 -> 0, of which waited for: 3 -> 0; matrix products, arithmetic and copies ran while one was open for 1% -> 0% of each run, Pallas kernels for 0% -> 0%
where the time goes in v1:
time: 284 us; the launch traced here: 283 us
  Pallas kernels  282 us (99%)
    pallas_call x1, Pallas kernels, on_lines(): pl.pallas_call(functools.partial(gather_kernel, n_zero, n_model), out_sha...  257 us
    pallas_call x1, Pallas kernels, on_lines(): pl.pallas_call(functools.partial(finish_kernel, d_model), grid=(d_model /...  25.1 us

profile of v1, /device:TPU:0, one launch (start us, length us, event | category | flops | bytes accessed | tf_op | source)
XLA Modules:
  0.0 283.3 jit_solution(8493485893440337856)
XLA Ops:
  0.6 257.0 %shard_map.162 = (bf16[4096,1024]{1,0:T(8,128)(2,1)}, bf16[4096,1024]{1,0:T(8,128)(2,1)}, bf16[4096,1024]{1,0:T(8,128)(2,1)}, bf16[8,48,512]{2,1,0:T(8,128)(2,1)...) custom-call(bf16[512,1024]{1,0:T(8,128)(2,1)} %w_q.1, bf16[512,1024]{1,0:T(8,128)(2,1)} %w_k.1, bf16[512,1024]{1,0:T(8,128)(2,1)} %w_v.1, ...), custom_call_target="tpu_custom_call" | custom-call | tf_op jit(solution)/shard_map/pallas_call | solution.py:278
  257.6 0.0 copy-start
  257.6 25.1 %shard_map.163 = (bf16[4096,1024]{1,0:T(8,128)(2,1)}, bf16[4096,1024]{1,0:T(8,128)(2,1)}, bf16[4096,1024]{1,0:T(8,128)(2,1)}, f32[1,1024]{1,0:T(1,128)}, f32[1,1024]{1,0:T(1,128)}, /*index=5*/f32[1,1024]{1,0:T(1,128)}) custom-call(bf16[4096,1024]{1,0:T(8,128)(2,1)} %get-tuple-element.19.g_q, bf16[4096,1024]{1,0:T(8,128)(2,1)} %get-tuple-element.20.g_k, ...), custom_call_target="tpu_custom_call" | custom-call | tf_op jit(solution)/shard_map/pallas_call | solution.py:312
  282.7 0.0 copy-done
  282.7 0.6 convert_reduce_fusion
Async XLA Ops:
  257.6 25.1 %copy-start = (f32[32,1,128]{2,1,0:T(1,128)S(1)}, f32[32,1,128]{2,1,0:T(1,128)}, u32[]{:S(2)}) copy-start(f32[32,1,128]{2,1,0:T(1,128)} %get-tuple-element.30) | copy-start | bytes 49156

commit v2 on v1

v2 whole, which is shorter than its diff:
```python
import functools

import jax
import jax.numpy as jnp
from jax import lax
from jax.experimental import pallas as pl
from jax.experimental.pallas import tpu as pltpu
from jax.sharding import PartitionSpec as P

MESH = pl.DeviceIdType.MESH
mix_rate = 0.5
VMEM_MOST = 67_043_328
SPARE = 65_536
COLUMNS = 2
PIECES = 6
WRITES = 4
FIRST = 2


def queues_of(z, length):
    every = [PIECES] + list(range(PIECES))
    late = list(range(PIECES // 2, PIECES))
    early = [c for c in every if c not in late]
    out = {"up": [], "down": [], "side": []}
    if z < length - 1:
        out["up"] += [(z - s, 0, c) for s in range(z + 1) for c in every]
        if z == 0:
            out["up"] += [(0, 1, c) for c in every]
        if z == length - 2:
            out["up"] += [(z, 1, c) for c in late]
    if z > 0:
        out["down"] += [(z + s, 0, c) for s in range(length - z) for c in every]
        if z == length - 1:
            out["down"] += [(z, 1, c) for c in every]
        if z == 1:
            out["down"] += [(z, 1, c) for c in late]
    for b in sorted(range(length), key=lambda b: (abs(b - z), b)):
        pieces = every
        if (z, b) in ((0, 1), (length - 1, length - 2)):
            pieces = early
        if (z, b) in ((1, 0), (length - 2, length - 1)):
            pieces = []
        out["side"] += [(b, 0, c) for c in pieces]
    return out


def order_of(length):
    size = [1.0] * PIECES + [0.1]
    queues = [queues_of(z, length) for z in range(length)]
    far = 1e9
    there = [{} for _ in range(length)]
    for z in range(length):
        for c in range(PIECES + 1):
            there[z][z, 0, c] = 0.0
    for _ in range(4 * length):
        for z in range(length):
            for name, queue in queues[z].items():
                now = 0.0
                for b, o, c in queue:
                    now = max(now, there[z].get((b, o, c), far)) + size[c]
                    to = {"up": z + 1, "down": z - 1, "side": z}[name]
                    key = (b, 1 - o if name == "side" else o, c)
                    there[to][key] = now
    result = []
    for z in range(length):
        events = []
        for name, queue in queues[z].items():
            key = 0.0
            for at, (b, o, c) in enumerate(queue):
                key = max(key, there[z][b, o, c])
                events.append((key, at, name, b, o, c))
        assert max(e[0] for e in events) < far
        result.append((sorted(events), there[z]))
    return result


def gather_kernel(
    n_zero, n_model,
    w_q, w_k, w_v, l_q, l_k, l_v, h_q, h_k, h_v, n_a, n_b,
    s_q, s_k, s_v, factors, norms, g_q, g_k, g_v,
    w_vm, h_vm, stage, lows, sums, scales, na_vm, nb_vm, ns_vm,
    send_sem, recv_sem, load_sem, store_sem, stage_sem, ssend_sem, srecv_sem, nsend_sem, nrecv_sem,
):
    w, low, high, gathered = (w_q, w_k, w_v), (l_q, l_k, l_v), (h_q, h_k, h_v), (g_q, g_k, g_v)
    served = (s_q, s_k, s_v)
    length = n_zero // COLUMNS
    zero, model = lax.axis_index("zero"), lax.axis_index("model")
    place, column = zero // COLUMNS, zero % COLUMNS
    rows, rank = w_q.shape[0], l_q.shape[0]
    half = rows // 2
    count = n_zero * n_model
    me = zero * n_model + model

    loads = []
    for m in range(3):
        into = lows.at[zero, pl.ds(m * rank, rank)]
        loads.append(pltpu.make_async_copy(low[m], into, load_sem.at[m]))
    for m in range(3):
        loads.append(pltpu.make_async_copy(w[m], w_vm.at[m], load_sem.at[3 + m]))
        loads.append(pltpu.make_async_copy(high[m], h_vm.at[m], load_sem.at[6 + m]))
    loads.append(pltpu.make_async_copy(n_a, na_vm, load_sem.at[9]))
    loads.append(pltpu.make_async_copy(n_b, nb_vm, load_sem.at[10]))
    for load in loads:
        load.start()

    barrier = pltpu.get_barrier_semaphore()

    def greet(k, carry):
        to = lax.rem(me + k, count)
        pl.semaphore_signal(
            barrier, inc=1, device_id=(to // n_model, to % n_model), device_id_type=MESH
        )
        return carry

    lax.fori_loop(1, count, greet, 0)
    pl.semaphore_wait(barrier, count - 1)
    for load in loads:
        load.wait()

    def block_at(b, o):
        return b * COLUMNS + (column if o == 0 else 1 - column)

    def landing(block, c):
        if c < PIECES:
            first = pl.multiple_of(block * rows, rows) + (c % 2) * half
            return gathered[c // 2].at[pl.ds(pl.multiple_of(first, half), half)]
        return lows.at[block]

    lane_of = {"up": 0, "down": 1, "side": 2}

    def copy_of(z, name, at, b, o, c):
        block = block_at(b, o)
        target = {
            "up": (z + 1) * COLUMNS + column,
            "down": (z - 1) * COLUMNS + column,
            "side": z * COLUMNS + 1 - column,
        }[name]
        source = landing(block, c)
        if b == z and o == 0 and c < PIECES:
            source = w[c // 2].at[pl.ds((c % 2) * half, half)]
        return pltpu.make_async_remote_copy(
            src_ref=source,
            dst_ref=landing(block, c),
            send_sem=send_sem.at[lane_of[name], at],
            recv_sem=recv_sem.at[block, c],
            device_id=(target, model),
            device_id_type=MESH,
        )

    def arrive(b, o, c):
        block = block_at(b, o)
        pltpu.make_async_copy(
            landing(block, c), landing(block, c), recv_sem.at[block, c]
        ).wait()

    def send_own(pieces):
        for z in range(length):

            @pl.when(place == z)
            def _(z=z):
                for key, at, name, b, o, c in orders[z][0]:
                    if b == z and o == 0 and c in pieces:
                        copy_of(z, name, at, b, o, c).start()

    orders = order_of(length)
    send_own((PIECES, *range(FIRST)))

    def whole_of(m, block, source, at):
        mixed = lax.dot_general(
            lows[block, pl.ds(m * rank, rank), at],
            h_vm[m],
            (((0,), (0,)), ((), ())),
            preferred_element_type=jnp.float32,
        )
        return source[at, :].astype(jnp.float32) + mix_rate * mixed

    tile = 128
    ns_vm[...] = na_vm[...] + nb_vm[...]
    for m in range(3):

        def add(i, total, m=m):
            at = pl.ds(pl.multiple_of(i * tile, tile), tile)
            whole = whole_of(m, zero, w_vm.at[m], at)
            return total + jnp.sum(
                jnp.abs(whole).reshape(tile // 8, 8, whole.shape[1]), axis=0
            )

        total = lax.fori_loop(
            0, rows // tile, add, jnp.zeros((8, w_vm.shape[2]), jnp.float32)
        )
        sums[zero, m : m + 1, :] = jnp.sum(total, axis=0, keepdims=True)

    def sum_copy(k):
        to = lax.rem(zero + k, n_zero)
        return pltpu.make_async_remote_copy(
            src_ref=sums.at[zero],
            dst_ref=sums.at[zero],
            send_sem=ssend_sem.at[k],
            recv_sem=srecv_sem.at[zero],
            device_id=(to, model),
            device_id_type=MESH,
        )

    def norm_copy(k):
        to = lax.rem(me + k, count)
        return pltpu.make_async_remote_copy(
            src_ref=ns_vm,
            dst_ref=norms.at[me],
            send_sem=nsend_sem.at[k],
            recv_sem=nrecv_sem.at[me],
            device_id=(to // n_model, to % n_model),
            device_id_type=MESH,
        )

    for k in range(1, n_zero):
        sum_copy(k).start()
    send_own(tuple(range(FIRST, PIECES)))

    def send_norm(k, carry):
        norm_copy(k).start()
        return carry

    lax.fori_loop(1, count, send_norm, 0)
    own_norm = pltpu.make_async_copy(ns_vm, norms.at[me], store_sem)
    own_norm.start()

    for k in range(1, n_zero):
        origin = lax.rem(zero + k, n_zero)
        pltpu.make_async_copy(sums.at[origin], sums.at[origin], srecv_sem.at[origin]).wait()
        sum_copy(k).wait_send()
    factor = jnp.sum(sums[...], axis=0) / (rows * n_zero)
    factors[...] = factor
    scales[...] = 1.0 / factor

    def finish(m, block, source):
        base = pl.multiple_of(block * rows, rows)

        def step(i, carry):
            first = pl.multiple_of(i * tile, tile)
            whole = whole_of(m, block, source, pl.ds(first, tile))
            to = pl.ds(pl.multiple_of(base + first, tile), tile)
            served[m][to, :] = (whole * scales[m : m + 1, :]).astype(s_q.dtype)
            return carry

        lax.fori_loop(0, rows // tile, step, 0)

    for m in range(3):
        finish(m, zero, w_vm.at[m])

    for z in range(length):

        @pl.when(place == z)
        def _(z=z):
            events, there = orders[z]
            items = [(key, 0, at, name, b, o, c) for key, at, name, b, o, c in events]
            for b in range(length):
                for o in range(COLUMNS):
                    if (b, o) != (z, 0):
                        for m in range(3):
                            when = max(there[b, o, c] for c in (2 * m, 2 * m + 1, PIECES))
                            items.append((when, 1, m, "", b, o, 0))
            seen = set()

            def need(b, o, c):
                if (b, o) != (z, 0) and (b, o, c) not in seen:
                    seen.add((b, o, c))
                    arrive(b, o, c)

            for _, kind, at, name, b, o, c in sorted(items):
                if kind == 0:
                    if (b, o) != (z, 0):
                        need(b, o, c)
                        copy_of(z, name, at, b, o, c).start()
                    continue
                for piece in (2 * at, 2 * at + 1, PIECES):
                    need(b, o, piece)
                block = block_at(b, o)
                raw = gathered[at].at[pl.ds(pl.multiple_of(block * rows, rows), rows)]
                load = pltpu.make_async_copy(raw, stage, stage_sem)
                load.start()
                load.wait()
                finish(at, block, stage)
            for key, at, name, b, o, c in events:
                copy_of(z, name, at, b, o, c).wait_send()

    own_norm.wait()

    def end_norm(k, carry):
        norm_copy(k).wait_send()
        origin = lax.rem(me + k, count)
        pltpu.make_async_copy(norms.at[origin], norms.at[origin], nrecv_sem.at[origin]).wait()
        return carry

    lax.fori_loop(1, count, end_norm, 0)


def write_kernel(s_q, s_k, s_v, factors, o_q, o_k, o_v, f_q, f_k, f_v, sem):
    rows = s_q.shape[0] // WRITES
    copies = []
    for m, (s, o) in enumerate(((s_q, o_q), (s_k, o_k), (s_v, o_v))):
        for i in range(WRITES):
            part = pl.ds(i * rows, rows)
            copies.append(pltpu.make_async_copy(s.at[part], o.at[part], sem.at[m * WRITES + i]))
            copies[-1].start()
    for m, f in enumerate((f_q, f_k, f_v)):
        f[...] = factors[m : m + 1, :]
    for copy in copies:
        copy.wait()


def on_lines(n_zero, n_model, w_q, l_q, h_q, w_k, l_k, h_k, w_v, l_v, h_v, n_a, n_b):
    rows, width = w_q.shape
    rank = l_q.shape[1]
    d_model = rows * n_zero
    count = n_zero * n_model
    share = n_a.shape[0]
    sends = (n_zero // COLUMNS) * (PIECES + 1) + PIECES
    f32, bf16 = jnp.float32, jnp.bfloat16
    shape = jax.ShapeDtypeStruct
    anywhere = pl.BlockSpec(memory_space=pl.ANY)
    inside = pl.BlockSpec(memory_space=pltpu.VMEM)
    dma = pltpu.SemaphoreType.DMA
    tall = (d_model, width)
    s_q, s_k, s_v, factors, norms, _, _, _ = pl.pallas_call(
        functools.partial(gather_kernel, n_zero, n_model),
        out_shape=(pltpu.VMEM(tall, bf16),) * 3
        + (shape((3, width), f32), shape((count, 1, share), f32))
        + (shape(tall, bf16),) * 3,
        in_specs=[anywhere] * 11,
        out_specs=(inside,) * 4 + (anywhere,) * 4,
        scratch_shapes=[
            pltpu.VMEM((3, rows, width), bf16),
            pltpu.VMEM((3, rank, width), bf16),
            pltpu.VMEM((rows, width), bf16),
            pltpu.VMEM((n_zero, 3 * rank, rows), bf16),
            pltpu.VMEM((n_zero, 3, width), f32),
            pltpu.VMEM((3, width), f32),
            pltpu.VMEM((1, share), f32),
            pltpu.VMEM((1, share), f32),
            pltpu.VMEM((1, share), f32),
            dma((3, sends)),
            dma((n_zero, PIECES + 1)),
            dma((11,)),
            dma,
            dma,
            dma((n_zero,)),
            dma((n_zero,)),
            dma((count,)),
            dma((count,)),
        ],
        compiler_params=pltpu.CompilerParams(
            collective_id=0, has_side_effects=True, vmem_limit_bytes=VMEM_MOST - 3 * d_model * width * 2 - SPARE
        ),
    )(w_q, w_k, w_v, l_q.T, l_k.T, l_v.T, h_q, h_k, h_v, n_a.reshape(1, share), n_b.reshape(1, share))
    *served, f_q, f_k, f_v = pl.pallas_call(
        write_kernel,
        out_shape=(shape(tall, bf16),) * 3 + (shape((1, width), f32),) * 3,
        in_specs=[anywhere] * 3 + [inside],
        out_specs=(anywhere,) * 3 + (inside,) * 3,
        scratch_shapes=[dma((3 * WRITES,))],
        compiler_params=pltpu.CompilerParams(
            vmem_limit_bytes=4 * 1024 * 1024
        ),
    )(s_q, s_k, s_v, factors)
    norm = norms.astype(bf16).reshape(count * share)
    return (*served, f_q.reshape(width), f_k.reshape(width), f_v.reshape(width), norm)


def plain(n_zero, n_model, w_q, l_q, h_q, w_k, l_k, h_k, w_v, l_v, h_v, n_a, n_b):
    d_model = w_q.shape[0] * n_zero
    wholes = [
        w.astype(jnp.float32) + mix_rate * jnp.dot(l, h, preferred_element_type=jnp.float32)
        for w, l, h in ((w_q, l_q, h_q), (w_k, l_k, h_k), (w_v, l_v, h_v))
    ]
    totals = lax.psum([jnp.sum(jnp.abs(whole), axis=0) for whole in wholes], "zero")
    factors = [total / d_model for total in totals]
    serving = [
        lax.all_gather((whole / factor).astype(jnp.bfloat16), "zero", axis=0, tiled=True)
        for whole, factor in zip(wholes, factors)
    ]
    norm = lax.all_gather(
        (n_a + n_b).astype(jnp.bfloat16), ("zero", "model"), axis=0, tiled=True
    )
    return (*serving, *factors, norm)


def solution(mesh):
    n_zero, n_model = mesh.shape["zero"], mesh.shape["model"]
    lines = n_zero == 2 * n_model
    tall, low, wide = P("zero", "model"), P("zero", None), P(None, "model")
    return jax.shard_map(
        functools.partial(on_lines if lines else plain, n_zero, n_model),
        mesh=mesh,
        in_specs=(tall, low, wide) * 3 + (P(("zero", "model")),) * 2,
        out_specs=(wide,) * 3 + (P("model"),) * 3 + (P(),),
        check_vma=False,
    )
```

time: 284 us -> 271 us (0.954)
  Pallas kernels: 282 us -> 268 us
    pallas_call x1, Pallas kernels: 25.1 us -> 9.08 us  [on_lines(): pl.pallas_call(write_kernel, out_shape=(shape(tall, bf16),) * 3 + (shape(...]
where the time goes in v2:
time: 271 us; the launch traced here: 270 us
  Pallas kernels  268 us (99%)
    pallas_call x1, Pallas kernels, on_lines(): pl.pallas_call(functools.partial(gather_kernel, n_zero, n_model), out_sha...  258 us
    pallas_call x1, Pallas kernels, on_lines(): pl.pallas_call(write_kernel, out_shape=(shape(tall, bf16),) * 3 + (shape(...  9.08 us

profile of v2, /device:TPU:0, one launch (start us, length us, event | category | flops | bytes accessed | tf_op | source)
XLA Modules:
  0.0 269.6 jit_solution(8408627951677945322)
XLA Ops:
  0.6 258.5 %shard_map.162 = (bf16[4096,1024]{1,0:T(8,128)(2,1)S(1)}, bf16[4096,1024]{1,0:T(8,128)(2,1)S(1)}, bf16[4096,1024]{1,0:T(8,128)(2,1)S(1)}, f32[3,1024]{1,0:T(4,12...) custom-call(bf16[512,1024]{1,0:T(8,128)(2,1)} %w_q.1, ...), custom_call_target="tpu_custom_call" | custom-call | tf_op jit(solution)/shard_map/pallas_call | solution.py:324
  259.1 0.0 copy-start
  259.1 0.7 copy-done
  259.8 0.0 copy-start.1
  259.8 9.1 %shard_map.163 = (bf16[4096,1024]{1,0:T(8,128)(2,1)}, bf16[4096,1024]{1,0:T(8,128)(2,1)}, bf16[4096,1024]{1,0:T(8,128)(2,1)}, f32[1,1024]{1,0:T(1,128)}, f32[1,1024]{1,0:T(1,128)}, /*index=5*/f32[1,1024]{1,0:T(1,128)}) custom-call(bf16[4096,1024]{1,0:T(8,128)(2,1)S(1)} %get-tuple-element.18.s_q, bf16[4096,1024]{1,0:T(8,128)(2,1)S(1)} %get-tuple-element.19.s_k, ...), custom_call_target="tpu_custom_call" | custom-call | tf_op jit(solution)/shard_map/pallas_call | solution.py:355
  268.9 0.0 copy-done.1
  268.9 0.6 convert_reduce_fusion
Async XLA Ops:
  259.1 0.7 copy-start
  259.8 9.1 %copy-start.1 = (f32[32,1,128]{2,1,0:T(1,128)S(1)}, f32[32,1,128]{2,1,0:T(1,128)}, u32[]{:S(2)}) copy-start(f32[32,1,128]{2,1,0:T(1,128)} %get-tuple-element.28) | copy-start | bytes 49156
